TPU v7x, 32 devices: a whole 2x2x4 slice. The times are simulated.
32 devices in a mesh: ctx: 16 (over z, x, core), wa: 2 (over y).
Axes of the slice: x: 2, y: 2, z: 4, core: 2. Of those that a mesh axis runs over, the one named last changes fastest.
Arguments:
- tokens: bfloat16 [2, 6144, 768], P('wa', 'ctx'), may hold values from -6 to 6
- cotangent: bfloat16 [2, 6144, 768], P('wa', 'ctx'), may hold values from -6 to 6
- lengths: int32 [2, 3], P('wa'), may hold values from 1024 to 3072, as said below
- block_order: int32 [32], replicated, may hold values from 0 to 31, each once
- w_query: float32 [768, 768], P('wa'), may hold values from -0.21875 to 0.21875
- b_query: float32 [768], P('wa'), may hold values from -4 to 4
- w_key: float32 [768, 768], P('wa'), may hold values from -0.21875 to 0.21875
- w_value: float32 [768, 768], P('wa'), may hold values from -0.21875 to 0.21875
- b_value: float32 [768], P('wa'), may hold values from -4 to 4
- w_out: float32 [768, 768], P('wa'), may hold values from -6 to 6
- b_out: float32 [768], P('wa'), may hold values from -4 to 4
- gain_one: float32 [768], P('wa'), may hold values from 0.5 to 1.5
- shift_one: float32 [768], P('wa'), may hold values from -4 to 4
- w_up: float32 [768, 3072], P('wa'), may hold values from -0.21875 to 0.21875
- b_up: float32 [3072], P('wa'), may hold values from -4 to 4
- w_down: float32 [3072, 768], P('wa'), may hold values from -0.109375 to 0.109375
- b_down: float32 [768], P('wa'), may hold values from -4 to 4
- gain_two: float32 [768], P('wa'), may hold values from 0.5 to 1.5
- shift_two: float32 [768], P('wa'), may hold values from -4 to 4
Outputs:
- activations: bfloat16 [2, 6144, 768], P('wa', 'ctx')
- input_grad: bfloat16 [2, 6144, 768], P('wa', 'ctx')
- grad_w_query: float32 [768, 768], P('wa')
- grad_b_query: float32 [768], P('wa')
- grad_w_key: float32 [768, 768], P('wa')
- grad_w_value: float32 [768, 768], P('wa')
- grad_b_value: float32 [768], P('wa')
- grad_w_out: float32 [768, 768], P('wa')
- grad_b_out: float32 [768], P('wa')
- grad_gain_one: float32 [768], P('wa')
- grad_shift_one: float32 [768], P('wa')
- grad_w_up: float32 [768, 3072], P('wa')
- grad_b_up: float32 [3072], P('wa')
- grad_w_down: float32 [3072, 768], P('wa')
- grad_b_down: float32 [768], P('wa')
- grad_gain_two: float32 [768], P('wa')
- grad_shift_two: float32 [768], P('wa')
Inputs may be any that keep to these rules, and one draw needn't show every extreme that they name: `lengths`: each slot holds three sequences, each of 1024 tokens or more, one of them exactly 3072; the rest of the slot, 2 tokens or more, is padding. `block_order`: each block number appears once.
All inputs are finite; a program needn't handle non-finite values.
Results may differ from a plain program's by a relative error of at most 0.023.
Values may be sent and summed in bfloat16 or wider, within the bound.
A program may use at most 256 MiB of HBM per device.

v0:
```python
from functools import partial
import jax
import jax.numpy as jnp
from jax import lax
from jax.sharding import PartitionSpec as P

HEADS = 12
HEAD_DIM = 64
epsilon = 1e-05


def layer_norm(hidden, gain_vec, shift_vec):
    centre = hidden - jnp.mean(hidden, axis=-1, keepdims=True)
    spread = jnp.mean(centre * centre, axis=-1, keepdims=True)
    return centre * lax.rsqrt(spread + epsilon) * gain_vec + shift_vec


def segment_of(position, seq_ends):
    return jnp.sum((position[:, None] >= seq_ends[None, :]).astype(jnp.int32), axis=1)


def segment_ids(row_ids, block_order, seq_ends, half_len):
    dealt_slot = row_ids // (2 * half_len) * 2 + row_ids // half_len % 2
    table_ids = jnp.arange(block_order.shape[0], dtype=jnp.int32)
    block_ids = jnp.sum(
        jnp.where(dealt_slot[:, None] == table_ids[None, :], block_order[None, :], 0), axis=1
    )
    position = block_ids * half_len + row_ids % half_len
    return segment_of(position, seq_ends)


def block_steps(tok_rows):
    return 2 * tok_rows


def body(
    tokens,
    cotangent,
    lengths,
    block_order,
    w_query,
    b_query,
    w_key,
    w_value,
    b_value,
    w_out,
    b_out,
    gain_one,
    shift_one,
    w_up,
    b_up,
    w_down,
    b_down,
    gain_two,
    shift_two,
):
    low_type = jnp.bfloat16
    inputs = tokens[0]
    tok_rows = inputs.shape[0]
    width = inputs.shape[1]
    half_len = tok_rows // 2
    seq_ends = jnp.cumsum(lengths[0])
    own_rows = lax.axis_index("ctx") * tok_rows + jnp.arange(tok_rows, dtype=jnp.int32)
    own_seg = segment_ids(own_rows, block_order, seq_ends, half_len)
    (
        query_weight,
        query_bias,
        key_weight,
        value_weight,
        value_bias,
        out_weight,
        out_bias,
        gain_first,
        shift_first,
    ) = (
        lax.all_gather(w_query.astype(low_type), "wa", axis=0, tiled=True),
        lax.all_gather(b_query.astype(low_type), "wa", axis=0, tiled=True),
        lax.all_gather(w_key.astype(low_type), "wa", axis=0, tiled=True),
        lax.all_gather(w_value.astype(low_type), "wa", axis=0, tiled=True),
        lax.all_gather(b_value.astype(low_type), "wa", axis=0, tiled=True),
        lax.all_gather(w_out.astype(low_type), "wa", axis=0, tiled=True),
        lax.all_gather(b_out.astype(low_type), "wa", axis=0, tiled=True),
        lax.all_gather(gain_one.astype(low_type), "wa", axis=0, tiled=True),
        lax.all_gather(shift_one.astype(low_type), "wa", axis=0, tiled=True),
    )
    query_proj = (
        ((jnp.dot(inputs, query_weight, preferred_element_type=jnp.float32) + query_bias) * 0.125)
        .astype(low_type)
        .reshape(tok_rows, HEADS, HEAD_DIM)
    )
    key_proj = (
        jnp.dot(inputs, key_weight, preferred_element_type=jnp.float32)
        .astype(low_type)
        .reshape(tok_rows, HEADS, HEAD_DIM)
    )
    value_proj = (
        (jnp.dot(inputs, value_weight, preferred_element_type=jnp.float32) + value_bias)
        .astype(low_type)
        .reshape(tok_rows, HEADS, HEAD_DIM)
    )

    def key_segments(first_row, block_num, step_rows):
        rows_now = first_row + block_num * step_rows + jnp.arange(step_rows, dtype=jnp.int32)
        return segment_ids(rows_now, block_order, seq_ends, half_len)

    def forward_block(state, key_blk, value_blk, key_seg):
        acc_sum, total = state
        scores = jnp.einsum("qhd,khd->hqk", query_proj, key_blk, preferred_element_type=jnp.float32)
        mask = own_seg[:, None] == key_seg[None, :]
        expo = jnp.where(mask[None], jnp.exp(scores), 0.0)
        total = total + jnp.sum(expo, axis=-1)
        acc_sum = acc_sum + jnp.einsum(
            "hqk,khd->qhd", expo.astype(low_type), value_blk, preferred_element_type=jnp.float32
        )
        return (acc_sum, total)

    start_state = (
        jnp.zeros((tok_rows, HEADS, HEAD_DIM), jnp.float32),
        jnp.zeros((HEADS, tok_rows), jnp.float32),
    )
    key_whole, value_whole = (
        lax.all_gather(key_proj, "ctx", axis=0, tiled=True),
        lax.all_gather(value_proj, "ctx", axis=0, tiled=True),
    )
    row_count = key_whole.shape[0]
    step_rows = block_steps(tok_rows)
    count = row_count // step_rows
    stacked = (
        key_whole.reshape(count, step_rows, HEADS, HEAD_DIM),
        value_whole.reshape(count, step_rows, HEADS, HEAD_DIM),
        jnp.arange(count, dtype=jnp.int32),
    )

    def advance(carry_state, scan_item):
        key_blk, value_blk, block_num = scan_item
        key_seg = key_segments(0, block_num, step_rows)
        fresh = forward_block(carry_state, key_blk, value_blk, key_seg)
        return (fresh, None)

    final_state, _ = lax.scan(advance, start_state, stacked)
    acc_sum, total = final_state
    context = acc_sum / total.T[:, :, None]
    context_low = context.astype(low_type).reshape(tok_rows, width)
    up_weight, up_bias, down_weight, down_bias, gain_second, shift_second = (
        lax.all_gather(w_up.astype(low_type), "wa", axis=0, tiled=True),
        lax.all_gather(b_up.astype(low_type), "wa", axis=0, tiled=True),
        lax.all_gather(w_down.astype(low_type), "wa", axis=0, tiled=True),
        lax.all_gather(b_down.astype(low_type), "wa", axis=0, tiled=True),
        lax.all_gather(gain_two.astype(low_type), "wa", axis=0, tiled=True),
        lax.all_gather(shift_two.astype(low_type), "wa", axis=0, tiled=True),
    )
    attn_out = jnp.dot(context_low, out_weight, preferred_element_type=jnp.float32) + out_bias
    h_one = inputs.astype(jnp.float32) + attn_out
    norm_one, norm_one_back = jax.vjp(
        layer_norm, h_one, gain_first.astype(jnp.float32), shift_first.astype(jnp.float32)
    )
    norm_low = norm_one.astype(low_type)
    up_pre = jnp.dot(norm_low, up_weight, preferred_element_type=jnp.float32) + up_bias
    gelu_out, gelu_back = jax.vjp(partial(jax.nn.gelu, approximate=False), up_pre)
    gelu_low = gelu_out.astype(low_type)
    down_out = jnp.dot(gelu_low, down_weight, preferred_element_type=jnp.float32) + down_bias
    h_two = norm_one + down_out
    result, norm_two_back = jax.vjp(
        layer_norm, h_two, gain_second.astype(jnp.float32), shift_second.astype(jnp.float32)
    )
    activations = result.astype(low_type)[None]
    valid = (own_seg < 3).astype(jnp.float32)
    g_out = cotangent[0].astype(jnp.float32) * valid[:, None]
    d_htwo, grad_gain_second, grad_shift_second = norm_two_back(g_out)
    d_down = d_htwo.astype(low_type)
    grad_wdown = jnp.einsum("tf,td->fd", gelu_low, d_down, preferred_element_type=jnp.float32)
    grad_bdown = jnp.sum(d_down.astype(jnp.float32), axis=0)
    d_gelu = jnp.einsum("td,fd->tf", d_down, down_weight, preferred_element_type=jnp.float32)
    (d_uppre,) = gelu_back(d_gelu)
    d_up = d_uppre.astype(low_type)
    grad_wup = jnp.einsum("td,tf->df", norm_low, d_up, preferred_element_type=jnp.float32)
    grad_bup = jnp.sum(d_up.astype(jnp.float32), axis=0)
    d_yone = d_htwo + jnp.einsum("tf,df->td", d_up, up_weight, preferred_element_type=jnp.float32)
    d_hone, grad_gain_first, grad_shift_first = norm_one_back(d_yone)
    d_attn = d_hone.astype(low_type)
    grad_wout = jnp.einsum("tc,td->cd", context_low, d_attn, preferred_element_type=jnp.float32)
    grad_bout = jnp.sum(d_attn.astype(jnp.float32), axis=0)
    d_context = jnp.einsum(
        "td,cd->tc", d_attn, out_weight, preferred_element_type=jnp.float32
    ).reshape(tok_rows, HEADS, HEAD_DIM)
    d_acc = (d_context / total.T[:, :, None]).astype(low_type)
    d_total = -jnp.sum(d_context * context, axis=-1).T / total

    def block_scores(key_blk, value_blk, key_seg):
        scores = jnp.einsum("qhd,khd->hqk", query_proj, key_blk, preferred_element_type=jnp.float32)
        mask = own_seg[:, None] == key_seg[None, :]
        expo = jnp.where(mask[None], jnp.exp(scores), 0.0)
        d_prob = jnp.einsum("qhd,khd->hqk", d_acc, value_blk, preferred_element_type=jnp.float32)
        d_scores = (expo * (d_prob + d_total[:, :, None])).astype(low_type)
        return (expo, d_scores)

    def backward_block(dq_sum, key_blk, value_blk, key_seg):
        expo, d_scores = block_scores(key_blk, value_blk, key_seg)
        dq_sum = dq_sum + jnp.einsum(
            "hqk,khd->qhd", d_scores, key_blk, preferred_element_type=jnp.float32
        )
        d_keyblk = jnp.einsum(
            "hqk,qhd->khd", d_scores, query_proj, preferred_element_type=jnp.float32
        )
        d_valueblk = jnp.einsum(
            "hqk,qhd->khd", expo.astype(low_type), d_acc, preferred_element_type=jnp.float32
        )
        return (dq_sum, (d_keyblk, d_valueblk))

    whole_rows = key_whole.shape[0]
    back_rows = 2 * tok_rows
    back_count = whole_rows // back_rows
    back_stack = (
        key_whole.reshape(back_count, back_rows, HEADS, HEAD_DIM),
        value_whole.reshape(back_count, back_rows, HEADS, HEAD_DIM),
        jnp.arange(back_count, dtype=jnp.int32),
    )
    dq_start = jnp.zeros((tok_rows, HEADS, HEAD_DIM), jnp.float32)

    def retreat(dq_sum, scan_item):
        key_blk, value_blk, block_num = scan_item
        key_seg = key_segments(0, block_num, back_rows)
        return backward_block(dq_sum, key_blk, value_blk, key_seg)

    dq_sum, (key_terms, value_terms) = lax.scan(retreat, dq_start, back_stack)
    key_terms = key_terms.reshape(whole_rows, HEADS, HEAD_DIM)
    value_terms = value_terms.reshape(whole_rows, HEADS, HEAD_DIM)
    key_sum, value_sum = (
        lax.psum_scatter(
            key_terms.astype(jnp.bfloat16), "ctx", scatter_dimension=0, tiled=True
        ).astype(jnp.float32),
        lax.psum_scatter(
            value_terms.astype(jnp.bfloat16), "ctx", scatter_dimension=0, tiled=True
        ).astype(jnp.float32),
    )
    d_keys = key_sum.astype(low_type).reshape(tok_rows, width)
    d_values = value_sum.astype(low_type).reshape(tok_rows, width)
    d_queries = (
        (dq_sum.astype(low_type).astype(jnp.float32) * 0.125)
        .astype(low_type)
        .reshape(tok_rows, width)
    )
    grad_wquery = jnp.einsum("tc,td->cd", inputs, d_queries, preferred_element_type=jnp.float32)
    grad_bquery = jnp.sum(d_queries.astype(jnp.float32), axis=0)
    grad_wkey = jnp.einsum("tc,td->cd", inputs, d_keys, preferred_element_type=jnp.float32)
    grad_wvalue = jnp.einsum("tc,td->cd", inputs, d_values, preferred_element_type=jnp.float32)
    grad_bvalue = jnp.sum(d_values.astype(jnp.float32), axis=0)
    d_input = d_hone + jnp.einsum(
        "td,cd->tc", d_queries, query_weight, preferred_element_type=jnp.float32
    )
    d_input = d_input + jnp.einsum(
        "td,cd->tc", d_keys, key_weight, preferred_element_type=jnp.float32
    )
    d_input = d_input + jnp.einsum(
        "td,cd->tc", d_values, value_weight, preferred_element_type=jnp.float32
    )
    input_grad = d_input.astype(low_type)[None]
    shards = (
        lax.psum_scatter(
            grad_wquery.astype(jnp.bfloat16), "wa", scatter_dimension=0, tiled=True
        ).astype(jnp.float32),
        lax.psum_scatter(
            grad_bquery.astype(jnp.bfloat16), "wa", scatter_dimension=0, tiled=True
        ).astype(jnp.float32),
        lax.psum_scatter(
            grad_wkey.astype(jnp.bfloat16), "wa", scatter_dimension=0, tiled=True
        ).astype(jnp.float32),
        lax.psum_scatter(
            grad_wvalue.astype(jnp.bfloat16), "wa", scatter_dimension=0, tiled=True
        ).astype(jnp.float32),
        lax.psum_scatter(
            grad_bvalue.astype(jnp.bfloat16), "wa", scatter_dimension=0, tiled=True
        ).astype(jnp.float32),
        lax.psum_scatter(
            grad_wout.astype(jnp.bfloat16), "wa", scatter_dimension=0, tiled=True
        ).astype(jnp.float32),
        lax.psum_scatter(
            grad_bout.astype(jnp.bfloat16), "wa", scatter_dimension=0, tiled=True
        ).astype(jnp.float32),
        lax.psum_scatter(
            grad_gain_first.astype(jnp.bfloat16), "wa", scatter_dimension=0, tiled=True
        ).astype(jnp.float32),
        lax.psum_scatter(
            grad_shift_first.astype(jnp.bfloat16), "wa", scatter_dimension=0, tiled=True
        ).astype(jnp.float32),
        lax.psum_scatter(
            grad_wup.astype(jnp.bfloat16), "wa", scatter_dimension=0, tiled=True
        ).astype(jnp.float32),
        lax.psum_scatter(
            grad_bup.astype(jnp.bfloat16), "wa", scatter_dimension=0, tiled=True
        ).astype(jnp.float32),
        lax.psum_scatter(
            grad_wdown.astype(jnp.bfloat16), "wa", scatter_dimension=0, tiled=True
        ).astype(jnp.float32),
        lax.psum_scatter(
            grad_bdown.astype(jnp.bfloat16), "wa", scatter_dimension=0, tiled=True
        ).astype(jnp.float32),
        lax.psum_scatter(
            grad_gain_second.astype(jnp.bfloat16), "wa", scatter_dimension=0, tiled=True
        ).astype(jnp.float32),
        lax.psum_scatter(
            grad_shift_second.astype(jnp.bfloat16), "wa", scatter_dimension=0, tiled=True
        ).astype(jnp.float32),
    )
    summed = (
        lax.psum(shards[0].astype(jnp.bfloat16), "ctx").astype(jnp.float32),
        lax.psum(shards[1].astype(jnp.bfloat16), "ctx").astype(jnp.float32),
        lax.psum(shards[2].astype(jnp.bfloat16), "ctx").astype(jnp.float32),
        lax.psum(shards[3].astype(jnp.bfloat16), "ctx").astype(jnp.float32),
        lax.psum(shards[4].astype(jnp.bfloat16), "ctx").astype(jnp.float32),
        lax.psum(shards[5].astype(jnp.bfloat16), "ctx").astype(jnp.float32),
        lax.psum(shards[6].astype(jnp.bfloat16), "ctx").astype(jnp.float32),
        lax.psum(shards[7].astype(jnp.bfloat16), "ctx").astype(jnp.float32),
        lax.psum(shards[8].astype(jnp.bfloat16), "ctx").astype(jnp.float32),
        lax.psum(shards[9].astype(jnp.bfloat16), "ctx").astype(jnp.float32),
        lax.psum(shards[10].astype(jnp.bfloat16), "ctx").astype(jnp.float32),
        lax.psum(shards[11].astype(jnp.bfloat16), "ctx").astype(jnp.float32),
        lax.psum(shards[12].astype(jnp.bfloat16), "ctx").astype(jnp.float32),
        lax.psum(shards[13].astype(jnp.bfloat16), "ctx").astype(jnp.float32),
        lax.psum(shards[14].astype(jnp.bfloat16), "ctx").astype(jnp.float32),
    )
    return (
        activations,
        input_grad,
        summed[0],
        summed[1],
        summed[2],
        summed[3],
        summed[4],
        summed[5],
        summed[6],
        summed[7],
        summed[8],
        summed[9],
        summed[10],
        summed[11],
        summed[12],
        summed[13],
        summed[14],
    )


def solution(mesh):
    placed = (
        P("wa", "ctx", None),
        P("wa", "ctx", None),
        P("wa", None),
        P(),
        P("wa", None),
        P("wa"),
        P("wa", None),
        P("wa", None),
        P("wa"),
        P("wa", None),
        P("wa"),
        P("wa"),
        P("wa"),
        P("wa", None),
        P("wa"),
        P("wa", None),
        P("wa"),
        P("wa"),
        P("wa"),
    )
    return jax.shard_map(
        body,
        mesh=mesh,
        in_specs=placed,
        out_specs=(
            P("wa", "ctx", None),
            P("wa", "ctx", None),
            P("wa", None),
            P("wa"),
            P("wa", None),
            P("wa", None),
            P("wa"),
            P("wa", None),
            P("wa"),
            P("wa"),
            P("wa"),
            P("wa", None),
            P("wa"),
            P("wa", None),
            P("wa"),
            P("wa"),
            P("wa"),
        ),
        check_vma=False,
    )
```

profile of v0, /device:TPU:0, one launch (start us, length us, event | category | flops | bytes accessed | tf_op | source)
XLA Modules:
  0.0 1424.4 jit_solution(14266771286409439732)
XLA Ops:
  16.9 18.7 %all-gather.18.cloned.1.call-done = bf16[768,768]{1,0:T(8,128)(2,1)} async-done(((bf16[384,768]{1,0:T(8,128)(2,1)}), bf16[768,768]{1,0:T(8,128)(2,1)}) %all-gather.18.cloned.1.call-update) | async-done | bytes 1179664 | tf_op jit(solution)/shard_map/all_gather | solution.py:79
  38.7 21.9 %all-gather.22.cloned.1.call-done = bf16[768,768]{1,0:T(8,128)(2,1)} async-done(((bf16[384,768]{1,0:T(8,128)(2,1)}), bf16[768,768]{1,0:T(8,128)(2,1)}) %all-gather.22.cloned.1.call-update) | async-done | bytes 1179664 | tf_op jit(solution)/shard_map/all_gather | solution.py:78
  111.9 60.1 %all-gather.20.cloned.1.call-done = bf16[6144,12,64]{0,2,1:T(8,128)(2,1)} async-done(((bf16[384,12,64]{0,2,1:T(8,128)(2,1)}), bf16[6144,12,64]{0,2,1:T(8,128)(2,1)}) %all-gather.20.cloned.1.call-update) | async-done | bytes 9437200 | tf_op jit(solution)/shard_map/all_gather | solution.py:123
  180.6 76.2 %all-gather.24.cloned.1.call-done = bf16[6144,12,64]{0,2,1:T(8,128)(2,1)} async-done(((bf16[384,12,64]{0,2,1:T(8,128)(2,1)}), bf16[6144,12,64]{0,2,1:T(8,128)(2,1)}) %all-gather.24.cloned.1.call-update) | async-done | bytes 9437200 | tf_op jit(solution)/shard_map/all_gather | solution.py:122
  265.5 153.1 %while.34 = (s32[]{:T(128)}, f32[384,12,64]{0,2,1:T(8,128)S(1)}, f32[12,384]{1,0:T(8,128)S(1)}, bf16[8,768,12,64]{1,3,2,0:T(8,128)(2,1)}, s32[384]{0:T(512)S(1)}...) while((s32[]{:T(128)}, f32[384,12,64]{0,2,1:T(8,128)S(1)}, ...), condition=%wide.region_7.8_spmd.clone, body=%wide.region_3.7_spmd.clone.sunk | while | flops 921122304 | bytes 34605872 | solution.py:140
  286.1 9.9 fusion.174
  305.8 9.0 fusion.174
  343.4 9.2 fusion.174
  352.6 9.7 fusion.175
  422.2 15.7 %multiply_convert_fusion = (bf16[384,3072]{1,0:T(8,128)(2,1)}, f32[384,3072]{1,0:T(8,128)}, f32[384,3072]{1,0:T(8,128)}) fusion(f32[3072]{0:T(1024)S(1)} %bitcast.223, bf16[768,3072]{1,0:T(8,128)(2,1)} %all-gather.30.cloned.1.call-done, f32[384,768]{1,0:T(8,128)S(1)} %get-tuple-element.736, f32[768]{0:T(1024)S(1)} %reshape.392, f32[768]{0:T(1024)S(1)} %reshape.391, ...), kind=kOutput, calls=%fused_computation.90 | convolution fusion | flops 1891270656 | bytes 17716224 | tf_op jit(solution)/shard_map/dot_general | solution.py:158
  460.1 282.4 %while.35 = (s32[]{:T(128)}, f32[384,12,64]{0,2,1:T(8,128)}, bf16[8,768,12,64]{1,3,2,0:T(8,128)(2,1)}, bf16[8,768,12,64]{1,3,2,0:T(8,128)(2,1)}, bf16[8,768,12,6...) while((s32[]{:T(128)}, f32[384,12,64]{0,2,1:T(8,128)}, ...), condition=%wide.region_20.21_spmd.clone, body=%wide.region_17.20_spmd.clone.sunk | while | flops 2287150080 | bytes 150747632 | solution.py:225
  465.7 9.2 fusion.189
  501.0 9.2 fusion.189
  536.2 9.2 fusion.189
  571.4 9.2 fusion.189
  606.7 9.2 fusion.189
  642.0 9.2 fusion.189
  677.2 9.2 fusion.189
  712.4 9.2 fusion.189
  742.6 28.1 %copy.113 = bf16[8,768,12,64]{3,2,1,0:T(8,128)(2,1)} copy(bf16[8,768,12,64]{1,3,2,0:T(8,128)(2,1)} %get-tuple-element.403) | data formatting | bytes 18874368
  770.7 30.0 %reshape.397 = bf16[6144,768]{1,0:T(8,128)(2,1)} reshape(bf16[6144,12,64]{2,1,0:T(8,128)(2,1)} %bitcast.205) | data formatting | bytes 18874368
  800.8 28.8 %copy.115 = bf16[8,768,12,64]{3,2,1,0:T(8,128)(2,1)} copy(bf16[8,768,12,64]{1,3,2,0:T(8,128)(2,1)} %get-tuple-element.404) | data formatting | bytes 18874368
  829.6 30.3 %reshape.399 = bf16[6144,768]{1,0:T(8,128)(2,1)} reshape(bf16[6144,12,64]{2,1,0:T(8,128)(2,1)} %bitcast.206) | data formatting | bytes 18874368
  863.7 47.4 %reduce-scatter.25.cloned.1.call-done = bf16[384,768]{1,0:T(8,128)(2,1)} async-done(((bf16[6144,768]{1,0:T(8,128)(2,1)}), bf16[384,768]{1,0:T(8,128)(2,1)}) %reduce-scatter.25.cloned.1.call-update) | async-done | bytes 589840 | tf_op jit(solution)/shard_map/reshape | solution.py:236
  914.4 111.4 %reduce-scatter.27.cloned.1.call-done = bf16[384,768]{1,0:T(8,128)(2,1)} async-done(((bf16[6144,768]{1,0:T(8,128)(2,1)}), bf16[384,768]{1,0:T(8,128)(2,1)}) %reduce-scatter.27.cloned.1.call-update) | async-done | bytes 589840 | tf_op jit(solution)/shard_map/reshape | solution.py:237
  1052.3 22.4 %reduce-scatter.31.cloned.1.call-done = bf16[384,768]{1,0:T(8,128)(2,1)} async-done(((bf16[768,768]{1,0:T(8,128)(2,1)}), bf16[384,768]{1,0:T(8,128)(2,1)}) %reduce-scatter.31.cloned.1.call-update) | async-done | bytes 589840
  1076.8 22.6 %reduce-scatter.33.cloned.1.call-done = bf16[384,768]{1,0:T(8,128)(2,1)} async-done(((bf16[768,768]{1,0:T(8,128)(2,1)}), bf16[384,768]{1,0:T(8,128)(2,1)}) %reduce-scatter.33.cloned.1.call-update) | async-done | bytes 589840
  1101.5 21.9 %reduce-scatter.19.cloned.1.call-done = bf16[384,768]{1,0:T(8,128)(2,1)} async-done(((bf16[768,768]{1,0:T(8,128)(2,1)}), bf16[384,768]{1,0:T(8,128)(2,1)}) %reduce-scatter.19.cloned.1.call-update) | async-done | bytes 589840 | tf_op jit(solution)/shard_map/reduce_scatter | solution.py:274
  1123.4 62.8 %reduce-scatter.21.cloned.1.call-done = bf16[384,3072]{1,0:T(8,128)(2,1)} async-done(((bf16[768,3072]{1,0:T(8,128)(2,1)}), bf16[384,3072]{1,0:T(8,128)(2,1)}) %reduce-scatter.21.cloned.1.call-update) | async-done | bytes 2359312 | tf_op jit(solution)/shard_map/reduce_scatter | solution.py:286
  1186.2 62.8 %reduce-scatter.23.cloned.1.call-done = bf16[1536,768]{1,0:T(8,128)(2,1)} async-done(((bf16[3072,768]{1,0:T(8,128)(2,1)}), bf16[1536,768]{1,0:T(8,128)(2,1)}) %reduce-scatter.23.cloned.1.call-update) | async-done | bytes 2359312 | tf_op jit(solution)/shard_map/reduce_scatter | solution.py:292
  1263.5 62.2 %all-reduce.9 = (bf16[384]{0:T(512)(128)(2,1)S(1)}, bf16[384]{0:T(512)(128)(2,1)S(1)}, bf16[384]{0:T(512)(128)(2,1)S(1)}, bf16[384]{0:T(512)(128)(2,1)S(1)}, bf1...) all-reduce(bf16[384]{0:T(512)(128)(2,1)S(1)} %dynamic-slice.1, ...), channel_id=1, replica_groups=mesh['ctx'=16,'wa'=2] {'ctx'}, use_global_device_ids=true, to_apply=%region_27.28 | all-reduce | flops 4608 | bytes 18432 | tf_op jit(solution)/shard_map/psum | solution.py:307
  1334.5 71.0 %all-reduce.14.cloned.1.call-done = (bf16[384,768]{0,1:T(8,128)(2,1)}, bf16[384,768]{0,1:T(8,128)(2,1)}, bf16[384,768]{0,1:T(8,128)(2,1)}, bf16[384,768]{1,0:T(8...) async-done(((bf16[384,768]{0,1:T(8,128)(2,1)}, bf16[384,768]{0,1:T(8,128)(2,1)}, bf16[384,768]{0,1:T(8,128)(2,1)}, bf16[384,768]{1,0:T(8,128)(2,1)}, ...) | async-done | bytes 7077904 | tf_op jit(solution)/shard_map/psum | solution.py:306
  (532 shorter events, 491.1 us)
Async XLA Ops:
  7.2 28.4 %all-gather.18.cloned.1.call-start = ((), (), s32[]{:S(2)}) async-start(), calls=%async_computation.8 | async-start | bytes 1769472 | tf_op jit(solution)/shard_map/all_gather | solution.py:79
  9.6 26.1 %copy-start.28 = (bf16[1,384,768]{2,1,0:T(8,128)(2,1)S(1)}, bf16[1,384,768]{2,1,0:T(8,128)(2,1)}, u32[]{:S(2)}) copy-start(bf16[1,384,768]{2,1,0:T(8,128)(2,1)} %param.23) | copy-start | bytes 1769476
  9.6 51.0 %all-gather.22.cloned.1.call-start = ((), (), s32[]{:S(2)}) async-start(), calls=%async_computation.10 | async-start | bytes 1769472 | tf_op jit(solution)/shard_map/all_gather | solution.py:78
  10.6 99.2 %all-gather.26.cloned.1.call-start = ((), (), s32[]{:S(2)}) async-start(), calls=%async_computation.12 | async-start | bytes 1769472 | tf_op jit(solution)/shard_map/all_gather | solution.py:76
  11.5 160.6 %all-gather.20.cloned.1.call-start = ((), (), s32[]{:S(2)}) async-start(), calls=%async_computation.9 | async-start | bytes 10027008 | tf_op jit(solution)/shard_map/all_gather | solution.py:123
  38.6 25.0 %copy-start.20 = (f32[384,768]{1,0:T(8,128)S(1)}, f32[384,768]{1,0:T(8,128)}, u32[]{:S(2)}) copy-start(f32[384,768]{1,0:T(8,128)} %param.32) | copy-start | bytes 3538948
  38.7 218.2 %all-gather.24.cloned.1.call-start = ((), (), s32[]{:S(2)}) async-start(), calls=%async_computation.11 | async-start | bytes 10027008 | tf_op jit(solution)/shard_map/all_gather | solution.py:122
  63.5 356.0 %all-gather.28.cloned.1.call-start = ((), (), s32[]{:S(2)}) async-start(), calls=%async_computation.13 | async-start | bytes 1769472 | tf_op jit(solution)/shard_map/all_gather | solution.py:81
  64.5 357.7 %all-gather.30.cloned.1.call-start = ((), (), s32[]{:S(2)}) async-start(), calls=%async_computation.14 | async-start | bytes 7077888 | tf_op jit(solution)/shard_map/all_gather | solution.py:145
  68.7 369.3 %all-gather.32.cloned.1.call-start = ((), (), s32[]{:S(2)}) async-start(), calls=%async_computation.15 | async-start | bytes 7077888 | tf_op jit(solution)/shard_map/all_gather | solution.py:147
  73.0 10.1 copy-start.48
  73.0 14.5 %copy-start.49 = (f32[384]{0:T(512)S(1)}, f32[384]{0:T(512)}, u32[]{:S(2)}) copy-start(f32[384]{0:T(512)} %param.35) | copy-start | bytes 4612
  73.0 18.9 %copy-start.42 = (f32[1536]{0:T(1024)S(1)}, f32[1536]{0:T(1024)}, u32[]{:S(2)}) copy-start(f32[1536]{0:T(1024)} %param.37) | copy-start | bytes 18436
  73.0 23.3 %copy-start.50 = (f32[384]{0:T(512)S(1)}, f32[384]{0:T(512)}, u32[]{:S(2)}) copy-start(f32[384]{0:T(512)} %param.39) | copy-start | bytes 4612
  73.0 27.8 %copy-start.51 = (f32[384]{0:T(512)S(1)}, f32[384]{0:T(512)}, u32[]{:S(2)}) copy-start(f32[384]{0:T(512)} %param.40) | copy-start | bytes 4612
  73.0 32.2 %copy-start.52 = (f32[384]{0:T(512)S(1)}, f32[384]{0:T(512)}, u32[]{:S(2)}) copy-start(f32[384]{0:T(512)} %param.41) | copy-start | bytes 4612
  73.1 838.0 %reduce-scatter.25.cloned.1.call-start = ((), (), s32[]{:S(2)}) async-start(), calls=%async_computation.19 | async-start | bytes 10027008 | tf_op jit(solution)/shard_map/reshape | solution.py:236
  87.5 368.4 %copy-start.35 = (f32[768]{0:T(1024)}, f32[768]{0:T(1024)S(1)}, u32[]{:S(2)}) copy-start(f32[768]{0:T(1024)S(1)} %reshape.391) | copy-start | bytes 9220
  91.9 346.1 %copy-start.43 = (f32[768]{0:T(1024)}, f32[768]{0:T(1024)S(1)}, u32[]{:S(2)}) copy-start(f32[768]{0:T(1024)S(1)} %reshape.392) | copy-start | bytes 9220
  421.9 34.0 %copy-start.11 = (f32[384,768]{1,0:T(8,128)}, f32[384,768]{1,0:T(8,128)S(1)}, u32[]{:S(2)}) copy-start(f32[384,768]{1,0:T(8,128)S(1)} %get-tuple-element.736) | copy-start | bytes 3538948
  421.9 34.0 %copy-start.33 = (f32[384]{0:T(512)}, f32[384]{0:T(512)S(1)}, u32[]{:S(2)}) copy-start(f32[384]{0:T(512)S(1)} %broadcast_multiply_fusion.1) | copy-start | bytes 4612
  422.2 33.7 %copy-start.37 = (f32[384]{0:T(512)}, f32[384]{0:T(512)S(1)}, u32[]{:S(2)}) copy-start(f32[384]{0:T(512)S(1)} %fusion.98) | copy-start | bytes 4612
  536.2 9.2 copy-start
  800.7 225.1 %reduce-scatter.27.cloned.1.call-start = ((), (), s32[]{:S(2)}) async-start(), calls=%async_computation.20 | async-start | bytes 10027008 | tf_op jit(solution)/shard_map/reshape | solution.py:237
  859.9 190.3 %reduce-scatter.29.cloned.1.call-start = ((), (), s32[]{:S(2)}) async-start(), calls=%async_computation.21 | async-start | bytes 1769472
  863.6 211.1 %reduce-scatter.31.cloned.1.call-start = ((), (), s32[]{:S(2)}) async-start(), calls=%async_computation.22 | async-start | bytes 1769472
  914.4 185.0 %reduce-scatter.33.cloned.1.call-start = ((), (), s32[]{:S(2)}) async-start(), calls=%async_computation.23 | async-start | bytes 1769472
  1029.3 94.1 %reduce-scatter.19.cloned.1.call-start = ((), (), s32[]{:S(2)}) async-start(), calls=%async_computation.16 | async-start | bytes 1769472 | tf_op jit(solution)/shard_map/reduce_scatter | solution.py:274
  1031.2 155.1 %reduce-scatter.21.cloned.1.call-start = ((), (), s32[]{:S(2)}) async-start(), calls=%async_computation.17 | async-start | bytes 7077888 | tf_op jit(solution)/shard_map/reduce_scatter | solution.py:286
  1037.5 211.5 %reduce-scatter.23.cloned.1.call-start = ((), (), s32[]{:S(2)}) async-start(), calls=%async_computation.18 | async-start | bytes 7077888 | tf_op jit(solution)/shard_map/reduce_scatter | solution.py:292
  1045.1 360.5 %all-reduce.14.cloned.1.call-start = ((), (), s32[]{:S(2)}) async-start(), calls=%async_computation.24 | async-start | bytes 14155776 | tf_op jit(solution)/shard_map/psum | solution.py:306
  1254.6 78.4 %copy-start.17 = (bf16[768,768]{1,0:T(8,128)(2,1)S(1)}, bf16[768,768]{1,0:T(8,128)(2,1)}, u32[]{:S(2)}) copy-start(bf16[768,768]{1,0:T(8,128)(2,1)} %all-gather.18.cloned.1.call-done) | copy-start | bytes 3538948
  (87 other events, 372.1 us)
Sparse Core Ops, SparseCore 0:
  10.1 25.4 all-gather.17
  37.8 22.7 all-gather.21
  62.7 22.8 all-gather.25
  88.1 83.8 all-gather.19
  174.7 82.0 all-gather.23
  258.8 20.9 all-gather.27
  281.9 62.6 all-gather.29
  346.1 62.6 all-gather.31
  800.9 110.1 reduce-scatter.24
  915.0 110.8 reduce-scatter.26
  1028.7 21.4 reduce-scatter.28
  1052.9 21.8 reduce-scatter.30
  1077.5 21.8 reduce-scatter.32
  1101.5 21.8 reduce-scatter.18
  1126.1 60.0 reduce-scatter.20
  1189.0 60.0 reduce-scatter.22
  1253.9 151.6 all-reduce.13
where the time goes:
time: 1430 us; the launch traced here: 1420 us
  waiting for transfers between devices  605 us (42%)
  matrix products  463 us (32%)
  local copies, waits for them, and re-layouts  176 us (12%)
  blocking collectives  111 us (8%)
  other arithmetic  42 us (3%)
  between operations  16.4 us (1%)
    unnamed x140, local copies, waits for them, and re-layouts  137 us
    reshape x1, waiting for transfers between devices, body(): d_values = value_sum.astype(low_type).reshape(tok_rows, width)  111 us
    all_gather x1, waiting for transfers between devices, body(): lax.all_gather(key_proj, 'ctx', axis=0, tiled=True)  76.2 us
    dot_general x8, matrix products, block_scores(): jnp.einsum('qhd,khd->hqk', d_acc, value_blk, preferred_element_type=jnp.f...  73.6 us
    dot_general x8, matrix products, forward_block(): jnp.einsum('qhd,khd->hqk', query_proj, key_blk, preferred_element_type=jn...  73.1 us
    psum x1, waiting for transfers between devices, body(): lax.psum(shards[0].astype(jnp.bfloat16), 'ctx').astype(jnp.float32)  71 us
    dot_general x8, matrix products, backward_block(): jnp.einsum('hqk,qhd->khd', expo.astype(low_type), d_acc, preferred_elemen...  68.4 us
    dot_general x8, matrix products, forward_block(): jnp.einsum('hqk,khd->qhd', expo.astype(low_type), value_blk, preferred_el...  66 us
  transfers between devices with their start and end apart: 17, of which 13 were waited for; matrix products, arithmetic and copies ran while one was open for 21% of the time, Pallas kernels for 0%

commit v1 on v0

--- a/solution.py
+++ b/solution.py
@@ -303,7 +303,7 @@
         ).astype(jnp.float32),
     )
     summed = (
-        lax.psum(shards[0].astype(jnp.bfloat16), "ctx").astype(jnp.float32),
+        jnp.sum(lax.all_gather(shards[0].astype(jnp.bfloat16), "ctx"), axis=0).astype(jnp.float32),
         lax.psum(shards[1].astype(jnp.bfloat16), "ctx").astype(jnp.float32),
         lax.psum(shards[2].astype(jnp.bfloat16), "ctx").astype(jnp.float32),
         lax.psum(shards[3].astype(jnp.bfloat16), "ctx").astype(jnp.float32),

time: 1430 us -> 1520 us (1.063)
  waiting for transfers between devices: 605 us -> 672 us
    all_gather x0 -> x1, waiting for transfers between devices: none -> 75.9 us  [body(): lax.all_gather(shards[0].astype(jnp.bfloat16), 'ctx')]
    unnamed x140 -> x139, local copies, waits for them, and re-layouts: 137 us -> 147 us
    unnamed x20 -> x21, waiting for transfers between devices: 50.3 us -> 48.5 us
  transfers between devices with their start and end apart: 17 -> 18, of which waited for: 13 -> 14; matrix products, arithmetic and copies ran while one was open for 21% -> 21% of each run, Pallas kernels for 0% -> 0%
where the time goes in v1:
time: 1520 us; the launch traced here: 1510 us
  waiting for transfers between devices  672 us (44%)
  matrix products  463 us (30%)
  local copies, waits for them, and re-layouts  186 us (12%)
  blocking collectives  111 us (7%)
  other arithmetic  50.2 us (3%)
  between operations  16.9 us (1%)
    unnamed x139, local copies, waits for them, and re-layouts  147 us
    reshape x1, waiting for transfers between devices, body(): d_values = value_sum.astype(low_type).reshape(tok_rows, width)  111 us
    all_gather x1, waiting for transfers between devices, body(): lax.all_gather(key_proj, 'ctx', axis=0, tiled=True)  76.2 us
    all_gather x1, waiting for transfers between devices, body(): lax.all_gather(shards[0].astype(jnp.bfloat16), 'ctx')  75.9 us
    dot_general x8, matrix products, block_scores(): jnp.einsum('qhd,khd->hqk', d_acc, value_blk, preferred_element_type=jnp.f...  73.6 us
    dot_general x8, matrix products, forward_block(): jnp.einsum('qhd,khd->hqk', query_proj, key_blk, preferred_element_type=jn...  73.1 us
    dot_general x8, matrix products, backward_block(): jnp.einsum('hqk,qhd->khd', expo.astype(low_type), d_acc, preferred_elemen...  68.4 us
    dot_general x8, matrix products, forward_block(): jnp.einsum('hqk,khd->qhd', expo.astype(low_type), value_blk, preferred_el...  66 us
  transfers between devices with their start and end apart: 18, of which 14 were waited for; matrix products, arithmetic and copies ran while one was open for 21% of the time, Pallas kernels for 0%

profile of v1, /device:TPU:0, one launch (start us, length us, event | category | flops | bytes accessed | tf_op | source)
XLA Modules:
  0.0 1510.1 jit_solution(6264106471868190424)
XLA Ops:
  16.9 18.7 %all-gather.20.cloned.1.call-done = bf16[768,768]{1,0:T(8,128)(2,1)} async-done(((bf16[384,768]{1,0:T(8,128)(2,1)}), bf16[768,768]{1,0:T(8,128)(2,1)}) %all-gather.20.cloned.1.call-update) | async-done | bytes 1179664 | tf_op jit(solution)/shard_map/all_gather | solution.py:79
  38.7 21.9 %all-gather.24.cloned.1.call-done = bf16[768,768]{1,0:T(8,128)(2,1)} async-done(((bf16[384,768]{1,0:T(8,128)(2,1)}), bf16[768,768]{1,0:T(8,128)(2,1)}) %all-gather.24.cloned.1.call-update) | async-done | bytes 1179664 | tf_op jit(solution)/shard_map/all_gather | solution.py:78
  111.9 60.1 %all-gather.22.cloned.1.call-done = bf16[6144,12,64]{0,2,1:T(8,128)(2,1)} async-done(((bf16[384,12,64]{0,2,1:T(8,128)(2,1)}), bf16[6144,12,64]{0,2,1:T(8,128)(2,1)}) %all-gather.22.cloned.1.call-update) | async-done | bytes 9437200 | tf_op jit(solution)/shard_map/all_gather | solution.py:123
  180.6 76.2 %all-gather.26.cloned.1.call-done = bf16[6144,12,64]{0,2,1:T(8,128)(2,1)} async-done(((bf16[384,12,64]{0,2,1:T(8,128)(2,1)}), bf16[6144,12,64]{0,2,1:T(8,128)(2,1)}) %all-gather.26.cloned.1.call-update) | async-done | bytes 9437200 | tf_op jit(solution)/shard_map/all_gather | solution.py:122
  265.5 153.1 %while.34 = (s32[]{:T(128)}, f32[384,12,64]{0,2,1:T(8,128)S(1)}, f32[12,384]{1,0:T(8,128)S(1)}, bf16[8,768,12,64]{1,3,2,0:T(8,128)(2,1)}, s32[384]{0:T(512)S(1)}...) while((s32[]{:T(128)}, f32[384,12,64]{0,2,1:T(8,128)S(1)}, ...), condition=%wide.region_7.8_spmd.clone, body=%wide.region_3.7_spmd.clone.sunk | while | flops 921122304 | bytes 34605872 | solution.py:140
  286.2 9.9 fusion.174
  352.6 9.7 fusion.175
  422.3 15.9 %multiply_convert_fusion = (bf16[384,3072]{1,0:T(8,128)(2,1)}, f32[384,3072]{1,0:T(8,128)}, f32[384,3072]{1,0:T(8,128)}) fusion(f32[3072]{0:T(1024)S(1)} %bitcast.229, bf16[768,3072]{1,0:T(8,128)(2,1)} %all-gather.32.cloned.1.call-done, f32[384,768]{1,0:T(8,128)S(1)} %get-tuple-element.735, f32[768]{0:T(1024)S(1)} %reshape.393, f32[768]{0:T(1024)S(1)} %reshape.392, ...), kind=kOutput, calls=%fused_computation.91 | convolution fusion | flops 1891270656 | bytes 17716224 | tf_op jit(solution)/shard_map/dot_general | solution.py:158
  460.3 282.2 %while.35 = (s32[]{:T(128)}, f32[384,12,64]{0,2,1:T(8,128)}, bf16[8,768,12,64]{1,3,2,0:T(8,128)(2,1)}, bf16[8,768,12,64]{1,3,2,0:T(8,128)(2,1)}, bf16[8,768,12,6...) while((s32[]{:T(128)}, f32[384,12,64]{0,2,1:T(8,128)}, ...), condition=%wide.region_20.21_spmd.clone, body=%wide.region_17.20_spmd.clone.sunk | while | flops 2287150080 | bytes 150747632 | solution.py:225
  465.7 9.2 fusion.189
  501.0 9.2 fusion.189
  536.2 9.2 fusion.189
  571.4 9.2 fusion.189
  606.7 9.2 fusion.189
  641.9 9.2 fusion.189
  677.2 9.2 fusion.189
  712.4 9.2 fusion.189
  742.6 28.1 %copy.111 = bf16[8,768,12,64]{3,2,1,0:T(8,128)(2,1)} copy(bf16[8,768,12,64]{1,3,2,0:T(8,128)(2,1)} %get-tuple-element.403) | data formatting | bytes 18874368
  770.7 30.0 %reshape.398 = bf16[6144,768]{1,0:T(8,128)(2,1)} reshape(bf16[6144,12,64]{2,1,0:T(8,128)(2,1)} %bitcast.210) | data formatting | bytes 18874368
  800.8 28.8 %copy.113 = bf16[8,768,12,64]{3,2,1,0:T(8,128)(2,1)} copy(bf16[8,768,12,64]{1,3,2,0:T(8,128)(2,1)} %get-tuple-element.404) | data formatting | bytes 18874368
  829.6 30.3 %reshape.400 = bf16[6144,768]{1,0:T(8,128)(2,1)} reshape(bf16[6144,12,64]{2,1,0:T(8,128)(2,1)} %bitcast.211) | data formatting | bytes 18874368
  860.0 51.0 %reduce-scatter.25.cloned.1.call-done = bf16[384,768]{1,0:T(8,128)(2,1)} async-done(((bf16[6144,768]{1,0:T(8,128)(2,1)}), bf16[384,768]{1,0:T(8,128)(2,1)}) %reduce-scatter.25.cloned.1.call-update) | async-done | bytes 589840 | tf_op jit(solution)/shard_map/reshape | solution.py:236
  914.4 111.4 %reduce-scatter.27.cloned.1.call-done = bf16[384,768]{1,0:T(8,128)(2,1)} async-done(((bf16[6144,768]{1,0:T(8,128)(2,1)}), bf16[384,768]{1,0:T(8,128)(2,1)}) %reduce-scatter.27.cloned.1.call-update) | async-done | bytes 589840 | tf_op jit(solution)/shard_map/reshape | solution.py:237
  1052.3 22.4 %reduce-scatter.33.cloned.1.call-done = bf16[384,768]{1,0:T(8,128)(2,1)} async-done(((bf16[768,768]{1,0:T(8,128)(2,1)}), bf16[384,768]{1,0:T(8,128)(2,1)}) %reduce-scatter.33.cloned.1.call-update) | async-done | bytes 589840
  1076.8 22.0 %reduce-scatter.19.cloned.1.call-done = bf16[384,768]{1,0:T(8,128)(2,1)} async-done(((bf16[768,768]{1,0:T(8,128)(2,1)}), bf16[384,768]{1,0:T(8,128)(2,1)}) %reduce-scatter.19.cloned.1.call-update) | async-done | bytes 589840 | tf_op jit(solution)/shard_map/reduce_scatter | solution.py:274
  1098.8 62.9 %reduce-scatter.21.cloned.1.call-done = bf16[384,3072]{1,0:T(8,128)(2,1)} async-done(((bf16[768,3072]{1,0:T(8,128)(2,1)}), bf16[384,3072]{1,0:T(8,128)(2,1)}) %reduce-scatter.21.cloned.1.call-update) | async-done | bytes 2359312 | tf_op jit(solution)/shard_map/reduce_scatter | solution.py:286
  1161.6 62.8 %reduce-scatter.23.cloned.1.call-done = bf16[1536,768]{1,0:T(8,128)(2,1)} async-done(((bf16[3072,768]{1,0:T(8,128)(2,1)}), bf16[1536,768]{1,0:T(8,128)(2,1)}) %reduce-scatter.23.cloned.1.call-update) | async-done | bytes 2359312 | tf_op jit(solution)/shard_map/reduce_scatter | solution.py:292
  1224.5 24.4 %reduce-scatter.29.cloned.1.call-done = bf16[384,768]{1,0:T(8,128)(2,1)} async-done(((bf16[768,768]{1,0:T(8,128)(2,1)}), bf16[384,768]{1,0:T(8,128)(2,1)}) %reduce-scatter.29.cloned.1.call-update) | async-done | bytes 589840
  1264.9 62.2 %all-reduce.9 = (bf16[384]{0:T(512)(128)(2,1)S(1)}, bf16[384]{0:T(512)(128)(2,1)S(1)}, bf16[384]{0:T(512)(128)(2,1)S(1)}, bf16[384]{0:T(512)(128)(2,1)S(1)}, bf1...) all-reduce(bf16[384]{0:T(512)(128)(2,1)S(1)} %dynamic-slice.1, ...), channel_id=1, replica_groups=mesh['ctx'=16,'wa'=2] {'ctx'}, use_global_device_ids=true, to_apply=%region_27.28 | all-reduce | flops 4608 | bytes 18432 | tf_op jit(solution)/shard_map/psum | solution.py:307
  1336.1 60.8 %all-reduce.14.cloned.1.call-done = (bf16[384,768]{0,1:T(8,128)(2,1)}, bf16[384,768]{0,1:T(8,128)(2,1)}, bf16[384,768]{1,0:T(8,128)(2,1)}, bf16[384,3072]{1,0:T(8,128)(2,1)}, bf16[1536,768]{1,0:T(8,128)(2,1)}) async-done(((bf16[384,768]{0,1:T(8,128)(2,1)}, bf16[384,768]{0,1:T(8,128)(2,1)}, bf16[384,768]{1,0:T(8,128)(2,1)}, bf16[384,3072]{1,0:T(8,128)(2,1)}, bf16[1536,768]{1,0:T(8,128)(2,1)}), ...) | async-done | bytes 6488080 | tf_op jit(solution)/shard_map/psum | solution.py:308
  1407.6 75.9 %all-gather.36.cloned.1.call-done = bf16[6144,768]{0,1:T(8,128)(2,1)} async-done(((bf16[384,768]{0,1:T(8,128)(2,1)}), bf16[6144,768]{0,1:T(8,128)(2,1)}) %all-gather.36.cloned.1.call-update) | async-done | bytes 9437200 | tf_op jit(solution)/shard_map/all_gather | solution.py:306
  1483.5 9.9 copy.119
  (535 shorter events, 513.3 us)
Async XLA Ops:
  7.2 28.4 %all-gather.20.cloned.1.call-start = ((), (), s32[]{:S(2)}) async-start(), calls=%async_computation.8 | async-start | bytes 1769472 | tf_op jit(solution)/shard_map/all_gather | solution.py:79
  9.6 26.1 %copy-start.27 = (bf16[1,384,768]{2,1,0:T(8,128)(2,1)S(1)}, bf16[1,384,768]{2,1,0:T(8,128)(2,1)}, u32[]{:S(2)}) copy-start(bf16[1,384,768]{2,1,0:T(8,128)(2,1)} %param.23) | copy-start | bytes 1769476
  9.6 51.0 %all-gather.24.cloned.1.call-start = ((), (), s32[]{:S(2)}) async-start(), calls=%async_computation.10 | async-start | bytes 1769472 | tf_op jit(solution)/shard_map/all_gather | solution.py:78
  10.6 99.2 %all-gather.28.cloned.1.call-start = ((), (), s32[]{:S(2)}) async-start(), calls=%async_computation.12 | async-start | bytes 1769472 | tf_op jit(solution)/shard_map/all_gather | solution.py:76
  11.5 160.6 %all-gather.22.cloned.1.call-start = ((), (), s32[]{:S(2)}) async-start(), calls=%async_computation.9 | async-start | bytes 10027008 | tf_op jit(solution)/shard_map/all_gather | solution.py:123
  38.6 25.0 %copy-start.20 = (f32[384,768]{1,0:T(8,128)S(1)}, f32[384,768]{1,0:T(8,128)}, u32[]{:S(2)}) copy-start(f32[384,768]{1,0:T(8,128)} %param.32) | copy-start | bytes 3538948
  38.6 218.2 %all-gather.26.cloned.1.call-start = ((), (), s32[]{:S(2)}) async-start(), calls=%async_computation.11 | async-start | bytes 10027008 | tf_op jit(solution)/shard_map/all_gather | solution.py:122
  63.5 356.0 %all-gather.30.cloned.1.call-start = ((), (), s32[]{:S(2)}) async-start(), calls=%async_computation.13 | async-start | bytes 1769472 | tf_op jit(solution)/shard_map/all_gather | solution.py:81
  64.5 357.7 %all-gather.32.cloned.1.call-start = ((), (), s32[]{:S(2)}) async-start(), calls=%async_computation.14 | async-start | bytes 7077888 | tf_op jit(solution)/shard_map/all_gather | solution.py:145
  68.7 369.5 %all-gather.34.cloned.1.call-start = ((), (), s32[]{:S(2)}) async-start(), calls=%async_computation.15 | async-start | bytes 7077888 | tf_op jit(solution)/shard_map/all_gather | solution.py:147
  73.0 27.8 %copy-start.50 = (f32[384]{0:T(512)S(1)}, f32[384]{0:T(512)}, u32[]{:S(2)}) copy-start(f32[384]{0:T(512)} %param.40) | copy-start | bytes 4612
  73.0 32.2 %copy-start.51 = (f32[384]{0:T(512)S(1)}, f32[384]{0:T(512)}, u32[]{:S(2)}) copy-start(f32[384]{0:T(512)} %param.41) | copy-start | bytes 4612
  73.1 837.9 %reduce-scatter.25.cloned.1.call-start = ((), (), s32[]{:S(2)}) async-start(), calls=%async_computation.20 | async-start | bytes 10027008 | tf_op jit(solution)/shard_map/reshape | solution.py:236
  87.5 368.6 %copy-start.34 = (f32[768]{0:T(1024)}, f32[768]{0:T(1024)S(1)}, u32[]{:S(2)}) copy-start(f32[768]{0:T(1024)S(1)} %reshape.392) | copy-start | bytes 9220
  91.9 346.3 %copy-start.42 = (f32[768]{0:T(1024)}, f32[768]{0:T(1024)S(1)}, u32[]{:S(2)}) copy-start(f32[768]{0:T(1024)S(1)} %reshape.393) | copy-start | bytes 9220
  421.9 34.2 %copy-start.11 = (f32[384,768]{1,0:T(8,128)}, f32[384,768]{1,0:T(8,128)S(1)}, u32[]{:S(2)}) copy-start(f32[384,768]{1,0:T(8,128)S(1)} %get-tuple-element.735) | copy-start | bytes 3538948
  421.9 34.2 %copy-start.32 = (f32[384]{0:T(512)}, f32[384]{0:T(512)S(1)}, u32[]{:S(2)}) copy-start(f32[384]{0:T(512)S(1)} %broadcast_multiply_fusion.1) | copy-start | bytes 4612
  422.2 33.9 %copy-start.36 = (f32[384]{0:T(512)}, f32[384]{0:T(512)S(1)}, u32[]{:S(2)}) copy-start(f32[384]{0:T(512)S(1)} %fusion.98) | copy-start | bytes 4612
  800.7 225.1 %reduce-scatter.27.cloned.1.call-start = ((), (), s32[]{:S(2)}) async-start(), calls=%async_computation.21 | async-start | bytes 10027008 | tf_op jit(solution)/shard_map/reshape | solution.py:237
  859.9 51.1 %copy-start.28 = (bf16[1,384,768]{2,1,0:T(8,128)(2,1)S(1)}, bf16[1,384,768]{2,1,0:T(8,128)(2,1)}, u32[]{:S(2)}) copy-start(bf16[1,384,768]{2,1,0:T(8,128)(2,1)} %param.23) | copy-start | bytes 1769476
  859.9 190.3 %reduce-scatter.31.cloned.1.call-start = ((), (), s32[]{:S(2)}) async-start(), calls=%async_computation.23 | async-start | bytes 1769472
  914.3 160.3 %reduce-scatter.33.cloned.1.call-start = ((), (), s32[]{:S(2)}) async-start(), calls=%async_computation.24 | async-start | bytes 1769472
  1029.2 69.6 %reduce-scatter.19.cloned.1.call-start = ((), (), s32[]{:S(2)}) async-start(), calls=%async_computation.16 | async-start | bytes 1769472 | tf_op jit(solution)/shard_map/reduce_scatter | solution.py:274
  1031.1 130.5 %reduce-scatter.21.cloned.1.call-start = ((), (), s32[]{:S(2)}) async-start(), calls=%async_computation.17 | async-start | bytes 7077888 | tf_op jit(solution)/shard_map/reduce_scatter | solution.py:286
  1037.5 187.0 %reduce-scatter.23.cloned.1.call-start = ((), (), s32[]{:S(2)}) async-start(), calls=%async_computation.18 | async-start | bytes 7077888 | tf_op jit(solution)/shard_map/reduce_scatter | solution.py:292
  1045.0 203.9 %reduce-scatter.29.cloned.1.call-start = ((), (), s32[]{:S(2)}) async-start(), calls=%async_computation.22 | async-start | bytes 1769472
  1048.7 348.1 %all-reduce.14.cloned.1.call-start = ((), (), s32[]{:S(2)}) async-start(), calls=%async_computation.25 | async-start | bytes 12976128 | tf_op jit(solution)/shard_map/psum | solution.py:308
  1224.5 26.7 %copy-start.54 = (u32[32]{0:T(128)S(1)}, u32[32]{0:T(128)}, u32[]{:S(2)}) copy-start(u32[32]{0:T(128)} %constant.320) | copy-start | bytes 388
  1224.5 29.2 %copy-start.8 = (f32[384,768]{1,0:T(8,128)S(1)}, f32[384,768]{1,0:T(8,128)}, u32[]{:S(2)}) copy-start(f32[384,768]{1,0:T(8,128)} %copy-done.7) | copy-start | bytes 3538948
  1224.5 29.2 %copy-start.31 = (f32[384]{0:T(512)S(1)}, f32[384]{0:T(512)}, u32[]{:S(2)}) copy-start(f32[384]{0:T(512)} %copy-done.30) | copy-start | bytes 4612
  1224.5 259.0 %all-gather.36.cloned.1.call-start = ((), (), s32[]{:S(2)}) async-start(), calls=%async_computation.19 | async-start | bytes 10027008 | tf_op jit(solution)/shard_map/all_gather | solution.py:306
  1256.0 78.6 %copy-start.17 = (bf16[768,768]{1,0:T(8,128)(2,1)S(1)}, bf16[768,768]{1,0:T(8,128)(2,1)}, u32[]{:S(2)}) copy-start(bf16[768,768]{1,0:T(8,128)(2,1)} %all-gather.20.cloned.1.call-done) | copy-start | bytes 3538948
  (87 other events, 435.4 us)
Sparse Core Ops, SparseCore 0:
  10.1 25.4 all-gather.19
  37.8 22.7 all-gather.23
  62.7 22.8 all-gather.27
  88.1 83.8 all-gather.21
  174.7 82.0 all-gather.25
  258.8 20.9 all-gather.29
  281.9 62.6 all-gather.31
  346.1 62.6 all-gather.33
  800.8 110.0 reduce-scatter.24
  914.9 110.8 reduce-scatter.26
  1028.6 21.4 reduce-scatter.30
  1052.8 21.8 reduce-scatter.32
  1076.9 21.8 reduce-scatter.18
  1101.5 60.0 reduce-scatter.20
  1164.4 60.0 reduce-scatter.22
  1227.1 21.8 reduce-scatter.28
  1253.7 143.0 all-reduce.13
  1399.4 84.0 all-gather.35
